TPU v7x, 32 devices: a whole 2x2x4 slice. The times are simulated.
32 devices in a mesh: rep: 2 (over x), blk: 16 (over z, y, core).
Axes of the slice: x: 2, y: 2, z: 4, core: 2. Of those that a mesh axis runs over, the one named last changes fastest.
Arguments:
- positions: float32 [3, 8192], P(None, ('rep', 'blk')), parts along dimension 1, may hold values from 0 to 64
- forces: float32 [6, 3, 8192], P(None, None, ('rep', 'blk')), parts along dimension 2, may hold values from -6 to 6
- random_kicks: float32 [6, 3, 8192], P(None, None, ('rep', 'blk')), parts along dimension 2, may hold values from -4 to 4
- history_velocity: float32 [128, 3, 8192], P(None, None, ('rep', 'blk')), parts along dimension 2, may hold values from -6 to 6
- history_offset: float32 [128, 3, 8192], P(None, None, ('rep', 'blk')), parts along dimension 2, may hold values from -8 to 8
- lag_index: int32 [4096], P(('rep', 'blk')), parts along dimension 0, may hold values from 0 to 127
Outputs:
- final_positions: float32 [3, 8192], P(None, ('rep', 'blk')), parts along dimension 1
- velocity: float32 [3, 8192], P(None, ('rep', 'blk')), parts along dimension 1
- statistics: float32 [2, 4096], P(None, ('rep', 'blk')), parts along dimension 1
There are 2 independent parts, one for each index of `rep`. A program takes and returns all parts, laid end to end along the dimension named above; each array names one. Nothing has to cross between parts.
All inputs are finite; a program needn't handle non-finite values.
Results may differ from a plain program's by a relative error of at most 0.0003.
Values sent between devices are 32-bit elements; how exact they have to be, the bound alone decides.
A program may use at most 64 MiB of HBM per device.

v0:
```python
import math

import jax
import jax.numpy as jnp
from jax import lax
from jax.sharding import PartitionSpec as P

STEPS = 6


time_step = 0.05


def pair_coefs(targets, sources):
    separation = targets[:, None, :] - sources[:, :, None]
    dist_sq = jnp.sum(separation * separation, axis=0)
    dist_safe = jnp.where(dist_sq > 0.0, dist_sq, 1.0)
    inv_dist = lax.rsqrt(dist_safe)
    distance = dist_sq * inv_dist
    inv_sq = 1.0 / dist_safe
    far_mask = distance >= 2.0
    coef_iso = jnp.where(
        far_mask, 0.75 * inv_dist * (1.0 + 2.0 / 3.0 * inv_sq), 1.0 - 9.0 / 32.0 * distance
    )
    coef_dir = jnp.where(
        far_mask, 0.75 * inv_dist * (1.0 - 2.0 * inv_sq) * inv_sq, 3.0 / 32.0 * inv_dist
    )
    return (separation, coef_iso, coef_dir)


def pair_velocity(targets, sources, loads):
    separation, coef_iso, coef_dir = pair_coefs(targets, sources)
    projection = jnp.sum(separation * loads[:, :, None], axis=0)
    return jnp.sum(
        coef_iso[None] * loads[:, :, None] + (coef_dir * projection)[None] * separation, axis=1
    )


def blockwise(targets, sources, loads):
    source_count = sources.shape[1]
    row_count = math.gcd(source_count, 512)
    block_count = source_count // row_count
    source_blocks = sources.reshape(3, block_count, row_count).transpose(1, 0, 2)
    load_blocks = loads.reshape(3, block_count, row_count).transpose(1, 0, 2)

    def accumulate(running, source_block):
        return (running + pair_velocity(targets, source_block[0], source_block[1]), None)

    running, unused = lax.scan(
        accumulate, jnp.zeros(targets.shape, jnp.float32), (source_blocks, load_blocks)
    )
    return running


def local(positions, forces, random_kicks, history_velocity, history_offset, lag_index):
    places = positions
    velocity = jnp.zeros_like(positions)
    all_forces = lax.all_gather(forces, "blk", axis=2, tiled=True)
    for step_index in range(STEPS):
        targets = places
        step_forces = all_forces[step_index]
        velocity = blockwise(
            targets, lax.all_gather(targets, "blk", axis=1, tiled=True), step_forces
        )
        places = places + time_step * velocity + random_kicks[step_index]
    velocity_dot = jnp.sum(velocity[None] * history_velocity, axis=(1, 2))
    moved = places[None] - positions[None] - history_offset
    square_disp = jnp.sum(moved * moved, axis=(1, 2))
    frames = history_velocity.shape[0]
    sphere_total = jnp.float32(positions.shape[1] * lax.axis_size("blk"))
    every_lag = lax.all_gather(lag_index, "blk", axis=0, tiled=True)
    onehot = (every_lag[:, None] == jnp.arange(frames, dtype=jnp.int32)[None, :]).astype(
        jnp.float32
    )
    frame_table = jnp.stack([velocity_dot, square_disp], axis=0)
    local_terms = jnp.dot(
        frame_table, onehot.T, precision=lax.Precision.HIGHEST, preferred_element_type=jnp.float32
    )
    statistics = (
        lax.psum_scatter(local_terms, "blk", scatter_dimension=1, tiled=True) / sphere_total
    )
    return (places, velocity, statistics)


def solution(mesh):
    return jax.shard_map(
        local,
        mesh=mesh,
        in_specs=(
            P(None, ("rep", "blk")),
            P(None, None, ("rep", "blk")),
            P(None, None, ("rep", "blk")),
            P(None, None, ("rep", "blk")),
            P(None, None, ("rep", "blk")),
            P(("rep", "blk")),
        ),
        out_specs=(P(None, ("rep", "blk")), P(None, ("rep", "blk")), P(None, ("rep", "blk"))),
        check_vma=False,
    )
```

profile of v0, /device:TPU:0, one launch (start us, length us, event | category | flops | bytes accessed | tf_op | source)
XLA Modules:
  0.0 293.1 jit_solution(7134342505187755510)
XLA Ops:
  7.3 24.4 %all_gather.25 = f32[6,3,4096]{2,1,0:T(4,128)S(1)} all-gather(f32[6,3,256]{2,1,0:T(4,128)} %param.19), channel_id=1, replica_groups=mesh['rep'=2,'blk'=16] {'blk'}, dimensions={2}, use_global_device_ids=true | all-gather | bytes 313344 | tf_op jit(solution)/shard_map/all_gather | solution.py:58
  31.8 17.6 %all_gather.24 = f32[3,4096]{1,0:T(4,128)S(1)} all-gather(f32[3,256]{1,0:T(4,128)S(1)} %copy-done), channel_id=1, replica_groups=mesh['rep'=2,'blk'=16] {'blk'}, dimensions={1}, use_global_device_ids=true | all-gather | bytes 52224 | tf_op jit(solution)/shard_map/all_gather | solution.py:63
  49.4 11.2 %while.66 = (s32[]{:T(128)}, f32[3,256]{1,0:T(4,128)S(1)}, f32[3,256]{1,0:T(4,128)S(1)}, f32[8,3,512]{2,1,0:T(4,128)S(1)}, f32[8,3,512]{2,1,0:T(4,128)S(1)}, /*index=5*/s32[]{:T(128)}, s32[]{:T(128)}) while((s32[]{:T(128)}, f32[3,256]{1,0:T(4,128)S(1)}, f32[3,256]{1,0:T(4,128)S(1)}, f32[8,3,512]{2,1,0:T(4,128)S(1)}, ...), condition=%wide.region_4.5_spmd.clone, body=%wide.region_0.4_spmd.clone.sunk | while | flops 6161155 | bytes 4261979 | solution.py:49
  50.3 0.5 fusion.68
  51.7 0.5 fusion.68
  53.1 0.5 fusion.68
  54.5 0.5 fusion.68
  55.9 0.5 fusion.68
  57.3 0.5 fusion.68
  58.7 0.5 fusion.68
  60.1 0.5 fusion.68
  60.6 18.9 %all_gather.26 = f32[3,4096]{1,0:T(4,128)S(1)} all-gather(f32[3,256]{1,0:T(4,128)S(1)} %bitcast_add_fusion.5), channel_id=1, replica_groups=mesh['rep'=2,'blk'=16] {'blk'}, dimensions={1}, use_global_device_ids=true | all-gather | bytes 52224 | tf_op jit(solution)/shard_map/all_gather | solution.py:63
  79.5 11.2 %while.67 = (s32[]{:T(128)}, f32[3,256]{1,0:T(4,128)S(1)}, f32[3,256]{1,0:T(4,128)S(1)}, f32[8,3,512]{2,1,0:T(4,128)S(1)}, f32[8,3,512]{2,1,0:T(4,128)S(1)}, /*index=5*/s32[]{:T(128)}, s32[]{:T(128)}) while((s32[]{:T(128)}, f32[3,256]{1,0:T(4,128)S(1)}, f32[3,256]{1,0:T(4,128)S(1)}, f32[8,3,512]{2,1,0:T(4,128)S(1)}, ...), condition=%wide.region_9.10_spmd.clone, body=%wide.region_5.9_spmd.clone.sunk | while | flops 6161155 | bytes 4261979 | solution.py:49
  80.4 0.5 fusion.70
  81.8 0.5 fusion.70
  83.2 0.5 fusion.70
  84.6 0.5 fusion.70
  86.0 0.5 fusion.70
  87.4 0.5 fusion.70
  88.8 0.5 fusion.70
  90.2 0.5 fusion.70
  90.7 17.6 %all_gather.27 = f32[3,4096]{1,0:T(4,128)S(1)} all-gather(f32[3,256]{1,0:T(4,128)S(1)} %bitcast_add_fusion.4), channel_id=1, replica_groups=mesh['rep'=2,'blk'=16] {'blk'}, dimensions={1}, use_global_device_ids=true | all-gather | bytes 52224 | tf_op jit(solution)/shard_map/all_gather | solution.py:63
  108.3 11.2 %while.68 = (s32[]{:T(128)}, f32[3,256]{1,0:T(4,128)S(1)}, f32[3,256]{1,0:T(4,128)S(1)}, f32[8,3,512]{2,1,0:T(4,128)S(1)}, f32[8,3,512]{2,1,0:T(4,128)S(1)}, /*index=5*/s32[]{:T(128)}, s32[]{:T(128)}) while((s32[]{:T(128)}, f32[3,256]{1,0:T(4,128)S(1)}, f32[3,256]{1,0:T(4,128)S(1)}, f32[8,3,512]{2,1,0:T(4,128)S(1)}, ...), condition=%wide.region_14.15_spmd.clone, body=%wide.region_10.14_spmd.clone.sunk | while | flops 6161155 | bytes 4261979 | solution.py:49
  109.2 0.5 fusion.72
  110.6 0.5 fusion.72
  113.4 0.5 fusion.72
  114.8 0.5 fusion.72
  116.2 0.5 fusion.72
  119.5 18.9 %all_gather.28 = f32[3,4096]{1,0:T(4,128)S(1)} all-gather(f32[3,256]{1,0:T(4,128)S(1)} %bitcast_add_fusion.3), channel_id=1, replica_groups=mesh['rep'=2,'blk'=16] {'blk'}, dimensions={1}, use_global_device_ids=true | all-gather | bytes 52224 | tf_op jit(solution)/shard_map/all_gather | solution.py:63
  138.5 11.2 %while.69 = (s32[]{:T(128)}, f32[3,256]{1,0:T(4,128)S(1)}, f32[3,256]{1,0:T(4,128)S(1)}, f32[8,3,512]{2,1,0:T(4,128)S(1)}, f32[8,3,512]{2,1,0:T(4,128)S(1)}, /*index=5*/s32[]{:T(128)}, s32[]{:T(128)}) while((s32[]{:T(128)}, f32[3,256]{1,0:T(4,128)S(1)}, f32[3,256]{1,0:T(4,128)S(1)}, f32[8,3,512]{2,1,0:T(4,128)S(1)}, ...), condition=%wide.region_19.20_spmd.clone, body=%wide.region_15.19_spmd.clone.sunk | while | flops 6161155 | bytes 4261979 | solution.py:49
  139.3 0.5 fusion.74
  140.7 0.5 fusion.74
  142.1 0.5 fusion.74
  143.5 0.5 fusion.74
  144.9 0.5 fusion.74
  146.3 0.5 fusion.74
  147.7 0.5 fusion.74
  149.1 0.5 fusion.74
  149.6 17.6 %all_gather.29 = f32[3,4096]{1,0:T(4,128)S(1)} all-gather(f32[3,256]{1,0:T(4,128)S(1)} %bitcast_add_fusion.2), channel_id=1, replica_groups=mesh['rep'=2,'blk'=16] {'blk'}, dimensions={1}, use_global_device_ids=true | all-gather | bytes 52224 | tf_op jit(solution)/shard_map/all_gather | solution.py:63
  167.3 11.1 %while.70 = (s32[]{:T(128)}, f32[3,256]{1,0:T(4,128)S(1)}, f32[3,256]{1,0:T(4,128)S(1)}, f32[8,3,512]{2,1,0:T(4,128)S(1)}, f32[8,3,512]{2,1,0:T(4,128)S(1)}, /*index=5*/s32[]{:T(128)}, s32[]{:T(128)}) while((s32[]{:T(128)}, f32[3,256]{1,0:T(4,128)S(1)}, f32[3,256]{1,0:T(4,128)S(1)}, f32[8,3,512]{2,1,0:T(4,128)S(1)}, ...), condition=%wide.region_24.25_spmd.clone, body=%wide.region_20.24_spmd.clone.sunk | while | flops 6161155 | bytes 4261979 | solution.py:49
  178.4 18.9 %all_gather.30 = f32[3,4096]{1,0:T(4,128)S(1)} all-gather(f32[3,256]{1,0:T(4,128)S(1)} %bitcast_add_fusion.1), channel_id=1, replica_groups=mesh['rep'=2,'blk'=16] {'blk'}, dimensions={1}, use_global_device_ids=true | all-gather | bytes 52224 | tf_op jit(solution)/shard_map/all_gather | solution.py:63
  197.4 11.2 %while.71 = (s32[]{:T(128)}, f32[3,256]{1,0:T(4,128)S(1)}, f32[3,256]{1,0:T(4,128)S(1)}, f32[8,3,512]{2,1,0:T(4,128)S(1)}, f32[8,3,512]{2,1,0:T(4,128)S(1)}, /*index=5*/s32[]{:T(128)}, s32[]{:T(128)}) while((s32[]{:T(128)}, f32[3,256]{1,0:T(4,128)S(1)}, f32[3,256]{1,0:T(4,128)S(1)}, f32[8,3,512]{2,1,0:T(4,128)S(1)}, ...), condition=%wide.region_29.30_spmd.clone, body=%wide.region_25.29_spmd.clone.sunk | while | flops 6161155 | bytes 4261979 | solution.py:49
  208.5 0.6 fusion.53
  209.3 17.5 %all-gather = s32[16,1,128]{2,1,0:T(1,128)S(1)} all-gather(s32[1,1,128]{2,1,0:T(1,128)S(1)} %bitcast.108), channel_id=1, replica_groups=mesh['rep'=2,'blk'=16] {'blk'}, dimensions={0}, use_global_device_ids=true | all-gather | bytes 8704 | tf_op jit(solution)/shard_map/all_gather | solution.py:71
  226.8 1.7 convolution_bitcast_fusion
  228.6 56.2 %reduce-scatter.4.cloned.1.call-done = f32[128,2]{1,0:T(8,128)} async-done(((f32[2048,2]{1,0:T(8,128)}), f32[128,2]{1,0:T(8,128)}) %reduce-scatter.4.cloned.1.call-update) | async-done | bytes 1040
  284.8 0.9 copy.25
  285.7 0.6 broadcast_multiply_fusion
  (239 shorter events, 51.0 us)
Async XLA Ops:
  7.2 24.6 %copy-start = (f32[3,256]{1,0:T(4,128)S(1)}, f32[3,256]{1,0:T(4,128)}, u32[]{:S(2)}) copy-start(f32[3,256]{1,0:T(4,128)} %param.18) | copy-start | bytes 9220
  7.2 277.6 %reduce-scatter.4.cloned.1.call-start = ((), (), s32[]{:S(2)}) async-start(), calls=%async_computation.1 | async-start | bytes 1114112
  49.4 11.2 %copy-start.4 = (f32[6,3,256]{2,1,0:T(4,128)S(1)}, f32[6,3,256]{2,1,0:T(4,128)}, u32[]{:S(2)}) copy-start(f32[6,3,256]{2,1,0:T(4,128)} %param.20) | copy-start | bytes 55300
  197.3 11.8 %copy-start.1 = (f32[128,3,256]{2,0,1:T(8,128)S(1)}, f32[128,3,256]{2,0,1:T(8,128)}, u32[]{:S(2)}) copy-start(f32[128,3,256]{2,0,1:T(8,128)} %param.21) | copy-start | bytes 1179652
  197.3 11.9 %copy-start.5 = (s32[128]{0:T(128)S(1)}, s32[128]{0:T(128)}, u32[]{:S(2)}) copy-start(s32[128]{0:T(128)} %param.23) | copy-start | bytes 1540
  197.3 29.4 %copy-start.2 = (f32[128,3,256]{2,0,1:T(8,128)S(1)}, f32[128,3,256]{2,0,1:T(8,128)}, u32[]{:S(2)}) copy-start(f32[128,3,256]{2,0,1:T(8,128)} %param.22) | copy-start | bytes 1179652
  208.5 20.1 %copy-start.3 = (f32[3,256]{1,0:T(4,128)}, f32[3,256]{1,0:T(4,128)S(1)}, u32[]{:S(2)}) copy-start(f32[3,256]{1,0:T(4,128)S(1)} %get-tuple-element.163) | copy-start | bytes 9220
Sparse Core Ops, SparseCore 0:
  228.7 56.0 reduce-scatter.3
where the time goes:
time: 293 us
  blocking collectives  152 us (52%)
  other arithmetic  65.7 us (22%)
  waiting for transfers between devices  56.2 us (19%)
  between operations  14.2 us (5%)
    all_gather x6, blocking collectives, local(): lax.all_gather(targets, 'blk', axis=1, tiled=True)  110 us
    unnamed x2, waiting for transfers between devices  56.2 us
    all_gather x1, blocking collectives, local(): all_forces = lax.all_gather(forces, 'blk', axis=2, tiled=True)  24.4 us
    reduce_sum x48, other arithmetic, pair_velocity(): jnp.sum(coef_iso[None] * loads[:, :, None] + (coef_dir * projection)[None...  23.4 us
    reduce_sum x48, other arithmetic, pair_coefs(): dist_sq = jnp.sum(separation * separation, axis=0)  22.6 us
    select_n x48, other arithmetic, pair_coefs(): jnp.where(far_mask, 0.75 * inv_dist * (1.0 + 2.0 / 3.0 * inv_sq), 1.0 - 9...  17.6 us
    all_gather x1, blocking collectives, local(): every_lag = lax.all_gather(lag_index, 'blk', axis=0, tiled=True)  17.5 us
  transfers between devices with their start and end apart: 1, of which 1 were waited for; matrix products, arithmetic and copies ran while one was open for 0% of the time, Pallas kernels for 0%

commit v1 on v0

v1 whole, which is shorter than its diff:
```python
import functools

import jax
import jax.numpy as jnp
from jax import lax
from jax.experimental import pallas as pl
from jax.experimental.pallas import tpu as pltpu
from jax.sharding import PartitionSpec as P

TIME_STEP = 0.05
LANES = 128
ROWS = 64


def pieces(value):
    high = value.astype(jnp.bfloat16)
    rest = value - high.astype(jnp.float32)
    mid = rest.astype(jnp.bfloat16)
    low = (rest - mid.astype(jnp.float32)).astype(jnp.bfloat16)
    return (high, mid, low)


def lane_sums(value):
    ones = jnp.ones((8, value.shape[1]), jnp.bfloat16)
    total = None
    for piece in pieces(value):
        term = lax.dot_general(
            ones, piece, (((1,), (1,)), ((), ())), preferred_element_type=jnp.float32
        )
        total = term if total is None else total + term
    return total


def kernel(
    n, steps, pos_ref, force_ref, kick_ref, hv_ref, ho_ref, lag_ref,
    out_pos, out_vel, out_stat,
    places, loads, cols, acc, hv, ho, table, tables,
    send_sem, recv_sem, fsend_sem, frecv_sem, tsend_sem, trecv_sem, hist_sem,
):
    me = lax.axis_index("blk")
    width = pos_ref.shape[1]
    tiles = width // LANES
    frames = hv_ref.shape[1]

    def partner(index):
        far = (index + 1) // 2
        sign = 2 * (index % 2) - 1
        return lax.rem(me + far * sign + n, n)

    def other(index):
        far = (index + 1) // 2
        sign = 2 * (index % 2) - 1
        return lax.rem(me - far * sign + n, n)

    get_hv = pltpu.make_async_copy(hv_ref, hv, hist_sem.at[0])
    get_ho = pltpu.make_async_copy(ho_ref, ho, hist_sem.at[1])
    get_hv.start()
    get_ho.start()

    barrier = pltpu.get_barrier_semaphore()

    @pl.loop(1, n)
    def _(index):
        pl.semaphore_signal(barrier, inc=1, device_id={"blk": partner(index)})

    def place_copy(step, owner, target):
        return pltpu.make_async_remote_copy(
            src_ref=places.at[step, me],
            dst_ref=places.at[step, owner],
            send_sem=send_sem.at[target],
            recv_sem=recv_sem.at[lax.rem(step, 2), owner],
            device_id={"blk": target},
        )

    def load_copy(owner, target):
        return pltpu.make_async_remote_copy(
            src_ref=loads.at[me],
            dst_ref=loads.at[owner],
            send_sem=fsend_sem.at[target],
            recv_sem=frecv_sem.at[owner],
            device_id={"blk": target},
        )

    def table_copy(owner, target):
        return pltpu.make_async_remote_copy(
            src_ref=table,
            dst_ref=tables.at[owner],
            send_sem=tsend_sem.at[target],
            recv_sem=trecv_sem.at[owner],
            device_id={"blk": target},
        )

    loads[me] = force_ref[...]
    places[0, me] = pos_ref[...] * 0.5
    pl.semaphore_wait(barrier, n - 1)

    @pl.loop(1, n)
    def _(index):
        place_copy(0, me, partner(index)).start()
        load_copy(me, partner(index)).start()

    @pl.loop(0, steps)
    def _(step):
        mine = places[step, me]
        padded = jnp.concatenate([mine, jnp.zeros((5, width), jnp.float32)], axis=0)
        turned = jnp.transpose(padded)
        for comp in range(3):
            cols[comp] = jnp.broadcast_to(turned[:, comp : comp + 1], (width, LANES))
            acc[comp] = jnp.zeros((width, LANES), jnp.float32)

        @pl.loop(0, n)
        def _(index):
            source = partner(index)

            @pl.when(index > 0)
            def _():
                place_copy(step, source, source).wait_recv()

            @pl.when(jnp.logical_and(index > 0, step == 0))
            def _():
                load_copy(source, source).wait_recv()

            @pl.loop(0, width // ROWS)
            def _(chunk):
                rows = pl.ds(pl.multiple_of(chunk * ROWS, ROWS), ROWS)
                target = [cols[comp, rows, :] for comp in range(3)]
                sums = [acc[comp, rows, :] for comp in range(3)]
                for tile in range(tiles):
                    lanes = pl.ds(tile * LANES, LANES)
                    sep = [
                        target[comp] - places[step, source, pl.ds(comp, 1), lanes]
                        for comp in range(3)
                    ]
                    load = [
                        loads[source, step, pl.ds(comp, 1), lanes] for comp in range(3)
                    ]
                    dist_sq = sep[0] * sep[0] + sep[1] * sep[1] + sep[2] * sep[2]
                    dist_sq = jnp.maximum(dist_sq, 1e-30)
                    inv = lax.rsqrt(dist_sq)
                    cut = jnp.minimum(inv, 1.0)
                    cut_sq = cut * cut
                    near = jnp.maximum(1.0 - dist_sq * inv, 0.0)
                    iso = cut * (6.0 + cut_sq) + 9.0 * near
                    along = cut * cut_sq * (2.0 - cut_sq) + (inv - cut)
                    push = along * (
                        sep[0] * (3.0 * load[0])
                        + sep[1] * (3.0 * load[1])
                        + sep[2] * (3.0 * load[2])
                    )
                    for comp in range(3):
                        sums[comp] = sums[comp] + (iso * load[comp] + push * sep[comp])
                for comp in range(3):
                    acc[comp, rows, :] = sums[comp]

        vel = jnp.concatenate(
            [lane_sums(acc[comp])[0:1] for comp in range(3)], axis=0
        ) * (1.0 / 16.0)

        @pl.loop(1, n)
        def _(index):
            place_copy(step, me, partner(index)).wait_send()

        fresh = mine + (0.5 * TIME_STEP) * vel + 0.5 * kick_ref[step]
        out_vel[...] = vel

        @pl.when(step < steps - 1)
        def _():
            places[step + 1, me] = fresh

            @pl.loop(1, n)
            def _(index):
                place_copy(step + 1, me, partner(index)).start()

        @pl.when(step == steps - 1)
        def _():
            out_pos[...] = 2.0 * fresh

    @pl.loop(1, n)
    def _(index):
        load_copy(me, partner(index)).wait_send()

    get_hv.wait()
    get_ho.wait()
    vel = out_vel[...]
    moved = out_pos[...] - pos_ref[...]
    dot = jnp.zeros((frames, LANES), jnp.float32)
    square = jnp.zeros((frames, LANES), jnp.float32)
    for comp in range(3):
        for tile in range(tiles):
            lanes = slice(tile * LANES, (tile + 1) * LANES)
            dot = dot + vel[comp : comp + 1, lanes] * hv[comp, :, lanes]
            gap = moved[comp : comp + 1, lanes] - ho[comp, :, lanes]
            square = square + gap * gap
    table[...] = jnp.concatenate([lane_sums(dot)[0:1], lane_sums(square)[0:1]], axis=0)

    @pl.loop(1, n)
    def _(index):
        table_copy(me, partner(index)).start()

    onehot = (
        lax.broadcasted_iota(jnp.int32, (frames, lag_ref.shape[1]), 0) == lag_ref[...]
    ).astype(jnp.bfloat16)
    tables[me] = table[...]

    @pl.loop(1, n)
    def _(index):
        table_copy(partner(index), partner(index)).wait_recv()

    whole = tables[0]
    for index in range(1, n):
        whole = whole + tables[index]
    whole = jnp.concatenate([whole, jnp.zeros((6, frames), jnp.float32)], axis=0)
    stat = None
    for piece in pieces(whole):
        term = jnp.dot(piece, onehot, preferred_element_type=jnp.float32)
        stat = term if stat is None else stat + term
    out_stat[...] = stat[0:2] / jnp.float32(width * n)

    @pl.loop(1, n)
    def _(index):
        table_copy(me, partner(index)).wait_send()


def local(n, positions, forces, random_kicks, history_velocity, history_offset, lag_index):
    steps = forces.shape[0]
    width = positions.shape[1]
    frames = history_velocity.shape[0]
    lags = lag_index.shape[0]
    vmem = pl.BlockSpec(memory_space=pltpu.VMEM)
    hbm = pl.BlockSpec(memory_space=pl.ANY)
    return pl.pallas_call(
        functools.partial(kernel, n, steps),
        out_shape=(
            jax.ShapeDtypeStruct((3, width), jnp.float32),
            jax.ShapeDtypeStruct((3, width), jnp.float32),
            jax.ShapeDtypeStruct((2, lags), jnp.float32),
        ),
        in_specs=[vmem, vmem, vmem, hbm, hbm, vmem],
        out_specs=(vmem, vmem, vmem),
        scratch_shapes=[
            pltpu.VMEM((steps, n, 3, width), jnp.float32),
            pltpu.VMEM((n, steps, 3, width), jnp.float32),
            pltpu.VMEM((3, width, LANES), jnp.float32),
            pltpu.VMEM((3, width, LANES), jnp.float32),
            pltpu.VMEM((3, frames, width), jnp.float32),
            pltpu.VMEM((3, frames, width), jnp.float32),
            pltpu.VMEM((2, frames), jnp.float32),
            pltpu.VMEM((n, 2, frames), jnp.float32),
            pltpu.SemaphoreType.DMA((n,)),
            pltpu.SemaphoreType.DMA((2, n)),
            pltpu.SemaphoreType.DMA((n,)),
            pltpu.SemaphoreType.DMA((n,)),
            pltpu.SemaphoreType.DMA((n,)),
            pltpu.SemaphoreType.DMA((n,)),
            pltpu.SemaphoreType.DMA((2,)),
        ],
        compiler_params=pltpu.CompilerParams(collective_id=0, has_side_effects=True),
    )(
        positions,
        forces,
        random_kicks,
        history_velocity.transpose(1, 0, 2),
        history_offset.transpose(1, 0, 2),
        lag_index.reshape(1, lags),
    )


def solution(mesh):
    return jax.shard_map(
        functools.partial(local, mesh.shape["blk"]),
        mesh=mesh,
        in_specs=(
            P(None, ("rep", "blk")),
            P(None, None, ("rep", "blk")),
            P(None, None, ("rep", "blk")),
            P(None, None, ("rep", "blk")),
            P(None, None, ("rep", "blk")),
            P(("rep", "blk")),
        ),
        out_specs=(P(None, ("rep", "blk")), P(None, ("rep", "blk")), P(None, ("rep", "blk"))),
        check_vma=False,
    )
```

time: 293 us -> 79.1 us (0.27)
  blocking collectives: 152 us -> 0 us
  Pallas kernels: 0 us -> 75.6 us
  other arithmetic: 65.7 us -> 0 us
  waiting for transfers between devices: 56.2 us -> 0 us
  between operations: 14.2 us -> 0.65 us
    all_gather x8 -> x0, blocking collectives: 152 us -> none  [the longest x6 110 us: local(): lax.all_gather(targets, 'blk', axis=1, tiled=True)]
    pallas_call x0 -> x1, Pallas kernels: none -> 75.6 us  [local(): pl.pallas_call(functools.partial(kernel, n, steps), out_shape=(jax.ShapeD...]
    unnamed x2 -> x0, waiting for transfers between devices: 56.2 us -> none
    reduce_sum x98 -> x0, other arithmetic: 46.3 us -> none  [the longest x48 23.4 us: pair_velocity(): jnp.sum(coef_iso[None] * loads[:, :, None] + (coef_dir * projection)[None...]
    select_n x48 -> x0, other arithmetic: 17.6 us -> none  [pair_coefs(): jnp.where(far_mask, 0.75 * inv_dist * (1.0 + 2.0 / 3.0 * inv_sq), 1.0 - 9...]
  transfers between devices with their start and end apart: 1 -> 0, of which waited for: 1 -> 0; matrix products, arithmetic and copies ran while one was open for 0% -> 0% of each run, Pallas kernels for 0% -> 0%
where the time goes in v1:
time: 79.1 us; the launch traced here: 78.8 us
  Pallas kernels  75.6 us (96%)
  local copies, waits for them, and re-layouts  2.57 us (3%)
    pallas_call x1, Pallas kernels, local(): pl.pallas_call(functools.partial(kernel, n, steps), out_shape=(jax.ShapeD...  75.6 us
    unnamed x9, local copies, waits for them, and re-layouts  2.57 us

profile of v1, /device:TPU:0, one launch (start us, length us, event | category | flops | bytes accessed | tf_op | source)
XLA Modules:
  0.0 78.8 jit_solution(16548852341604049937)
XLA Ops:
  0.6 75.6 %shard_map.85 = (f32[3,256]{1,0:T(4,128)}, f32[3,256]{1,0:T(4,128)}, f32[2,128]{1,0:T(2,128)}) custom-call(f32[3,256]{1,0:T(4,128)} %pos_ref.1, f32[6,3,256]{2,1,0:T(4,128)} %force_ref.1, f32[6,3,256]{2,1,0:T(4,128)} %kick_ref.1, f32[3,128,256]{2,1,0:T(8,128)} %bitcast.3, f32[3,128,256]{2,1,0:T(8,128)} %bitcast.4, s32[1,128]{1,0:T(1,128)} %bitcast.5), custom_call_target="tpu_custom_call" | custom-call | tf_op jit(solution)/shard_map/pallas_call | solution.py:231
  76.3 0.0 copy-start.1
  76.3 0.7 copy-done.1
  76.9 0.0 copy-start
  76.9 0.6 copy.12
  77.5 0.1 copy-done
  77.6 0.0 copy-start.2
  77.6 0.6 copy.13
  78.2 0.1 copy-done.2
  78.3 0.6 copy.14
Async XLA Ops:
  76.3 0.7 copy-start.1
  76.9 0.7 copy-start
  77.6 0.7 copy-start.2

commit v2 on v1

--- a/solution.py
+++ b/solution.py
@@ -35,22 +35,34 @@
     n, steps, pos_ref, force_ref, kick_ref, hv_ref, ho_ref, lag_ref,
     out_pos, out_vel, out_stat,
     places, loads, cols, acc, hv, ho, table, tables,
-    send_sem, recv_sem, fsend_sem, frecv_sem, tsend_sem, trecv_sem, hist_sem,
+    send_sem, recv_sem, pass_sem, fsend_sem, frecv_sem, tsend_sem, trecv_sem, hist_sem,
 ):
     me = lax.axis_index("blk")
     width = pos_ref.shape[1]
     tiles = width // LANES
     frames = hv_ref.shape[1]
 
+    cores = 2 if n % 2 == 0 else 1
+    chips = n // cores
+    per = 2 if chips % 2 == 0 else 1
+    planes = chips // per
+    core, chip = me % cores, me // cores
+    plane, seat = chip // per, chip % per
+    edge = jnp.minimum(plane, planes - 1 - plane)
+    low = plane < planes - 1 - plane
+    twin = chip * cores + (core + 1) % cores
+
     def partner(index):
-        far = (index + 1) // 2
-        sign = 2 * (index % 2) - 1
-        return lax.rem(me + far * sign + n, n)
-
-    def other(index):
-        far = (index + 1) // 2
-        sign = 2 * (index % 2) - 1
-        return lax.rem(me - far * sign + n, n)
+        return lax.rem(me + index, n)
+
+    def chip_at(order):
+        hop, sub = order // per, order % per
+        far = jnp.where(hop <= 2 * edge, (hop + 1) // 2, hop - edge)
+        ahead = jnp.where(hop <= 2 * edge, hop % 2 == 1, low)
+        return (plane + jnp.where(ahead, far, -far)) * per + (seat + sub) % per
+
+    def peer(order):
+        return chip_at(order) * cores + core
 
     get_hv = pltpu.make_async_copy(hv_ref, hv, hist_sem.at[0])
     get_ho = pltpu.make_async_copy(ho_ref, ho, hist_sem.at[1])
@@ -63,23 +75,42 @@
     def _(index):
         pl.semaphore_signal(barrier, inc=1, device_id={"blk": partner(index)})
 
-    def place_copy(step, owner, target):
+    def place_copy(step, owner, target, sem):
         return pltpu.make_async_remote_copy(
-            src_ref=places.at[step, me],
+            src_ref=places.at[step, owner],
             dst_ref=places.at[step, owner],
-            send_sem=send_sem.at[target],
+            send_sem=sem,
             recv_sem=recv_sem.at[lax.rem(step, 2), owner],
             device_id={"blk": target},
         )
 
-    def load_copy(owner, target):
+    def load_copy(part, owner, target, sem):
+        first, count = ((0, 1), (1, steps - 1))[part]
         return pltpu.make_async_remote_copy(
-            src_ref=loads.at[me],
-            dst_ref=loads.at[owner],
-            send_sem=fsend_sem.at[target],
-            recv_sem=frecv_sem.at[owner],
+            src_ref=loads.at[owner, pl.ds(first, count)],
+            dst_ref=loads.at[owner, pl.ds(first, count)],
+            send_sem=sem,
+            recv_sem=frecv_sem.at[part, owner],
             device_id={"blk": target},
         )
+
+    def place_out(step, action):
+        if cores == 2:
+            getattr(place_copy(step, me, twin, send_sem.at[twin]), action)()
+
+        @pl.loop(1, chips)
+        def _(order):
+            to = peer(order)
+            getattr(place_copy(step, me, to, send_sem.at[to]), action)()
+
+    def load_out(part, action):
+        if cores == 2:
+            getattr(load_copy(part, me, twin, fsend_sem.at[part, twin]), action)()
+
+        @pl.loop(1, chips)
+        def _(order):
+            to = peer(order)
+            getattr(load_copy(part, me, to, fsend_sem.at[part, to]), action)()
 
     def table_copy(owner, target):
         return pltpu.make_async_remote_copy(
@@ -94,10 +125,10 @@
     places[0, me] = pos_ref[...] * 0.5
     pl.semaphore_wait(barrier, n - 1)
 
-    @pl.loop(1, n)
-    def _(index):
-        place_copy(0, me, partner(index)).start()
-        load_copy(me, partner(index)).start()
+    place_out(0, "start")
+    load_out(0, "start")
+    if steps > 1:
+        load_out(1, "start")
 
     @pl.loop(0, steps)
     def _(step):
@@ -110,15 +141,43 @@
 
         @pl.loop(0, n)
         def _(index):
-            source = partner(index)
+            if cores == 2:
+                direct = jnp.logical_or(
+                    index == 0, jnp.logical_and(index % 2 == 1, index < n - 1)
+                )
+                order = jnp.where(
+                    direct,
+                    (index + 1) // 2,
+                    jnp.where(index == n - 1, chips - 1, (index - 2) // 2),
+                )
+                side = jnp.where(direct, core, 1 - core)
+                source = chip_at(order) * cores + side
+                passing = jnp.logical_and(direct, index > 0)
+            else:
+                source = peer(index)
+                passing = None
 
             @pl.when(index > 0)
             def _():
-                place_copy(step, source, source).wait_recv()
-
-            @pl.when(jnp.logical_and(index > 0, step == 0))
-            def _():
-                load_copy(source, source).wait_recv()
+                place_copy(step, source, source, send_sem.at[source]).wait_recv()
+
+            if passing is not None:
+
+                @pl.when(passing)
+                def _():
+                    place_copy(step, source, twin, pass_sem.at[0, source]).start()
+
+            for part in range(min(2, steps)):
+
+                @pl.when(jnp.logical_and(index > 0, step == part))
+                def _():
+                    load_copy(part, source, source, fsend_sem.at[part, source]).wait_recv()
+
+                if passing is not None:
+
+                    @pl.when(jnp.logical_and(passing, step == part))
+                    def _():
+                        load_copy(part, source, twin, pass_sem.at[part + 1, source]).start()
 
             @pl.loop(0, width // ROWS)
             def _(chunk):
@@ -141,7 +200,8 @@
                     cut_sq = cut * cut
                     near = jnp.maximum(1.0 - dist_sq * inv, 0.0)
                     iso = cut * (6.0 + cut_sq) + 9.0 * near
-                    along = cut * cut_sq * (2.0 - cut_sq) + (inv - cut)
+                    rest = 1.0 - cut_sq
+                    along = inv - cut * (rest * rest)
                     push = along * (
                         sep[0] * (3.0 * load[0])
                         + sep[1] * (3.0 * load[1])
@@ -156,9 +216,13 @@
             [lane_sums(acc[comp])[0:1] for comp in range(3)], axis=0
         ) * (1.0 / 16.0)
 
-        @pl.loop(1, n)
-        def _(index):
-            place_copy(step, me, partner(index)).wait_send()
+        place_out(step, "wait_send")
+        if cores == 2:
+
+            @pl.loop(1, chips)
+            def _(order):
+                source = peer(order)
+                place_copy(step, source, twin, pass_sem.at[0, source]).wait_send()
 
         fresh = mine + (0.5 * TIME_STEP) * vel + 0.5 * kick_ref[step]
         out_vel[...] = vel
@@ -167,17 +231,20 @@
         def _():
             places[step + 1, me] = fresh
 
-            @pl.loop(1, n)
-            def _(index):
-                place_copy(step + 1, me, partner(index)).start()
+            place_out(step + 1, "start")
 
         @pl.when(step == steps - 1)
         def _():
             out_pos[...] = 2.0 * fresh
 
-    @pl.loop(1, n)
-    def _(index):
-        load_copy(me, partner(index)).wait_send()
+    for part in range(min(2, steps)):
+        load_out(part, "wait_send")
+        if cores == 2:
+
+            @pl.loop(1, chips)
+            def _(order):
+                source = peer(order)
+                load_copy(part, source, twin, pass_sem.at[part + 1, source]).wait_send()
 
     get_hv.wait()
     get_ho.wait()
@@ -248,8 +315,9 @@
             pltpu.VMEM((n, 2, frames), jnp.float32),
             pltpu.SemaphoreType.DMA((n,)),
             pltpu.SemaphoreType.DMA((2, n)),
-            pltpu.SemaphoreType.DMA((n,)),
-            pltpu.SemaphoreType.DMA((n,)),
+            pltpu.SemaphoreType.DMA((3, n)),
+            pltpu.SemaphoreType.DMA((2, n)),
+            pltpu.SemaphoreType.DMA((2, n)),
             pltpu.SemaphoreType.DMA((n,)),
             pltpu.SemaphoreType.DMA((n,)),
             pltpu.SemaphoreType.DMA((2,)),

time: 79.1 us -> 75.8 us (0.958)
  Pallas kernels: 75.6 us -> 72.3 us
    pallas_call x1, Pallas kernels: 75.6 us -> 72.3 us  [local(): pl.pallas_call(functools.partial(kernel, n, steps), out_shape=(jax.ShapeD...]
where the time goes in v2:
time: 75.8 us; the launch traced here: 75.5 us
  Pallas kernels  72.3 us (95%)
  local copies, waits for them, and re-layouts  2.57 us (3%)
    pallas_call x1, Pallas kernels, local(): pl.pallas_call(functools.partial(kernel, n, steps), out_shape=(jax.ShapeD...  72.3 us
    unnamed x9, local copies, waits for them, and re-layouts  2.57 us

profile of v2, /device:TPU:0, one launch (start us, length us, event | category | flops | bytes accessed | tf_op | source)
XLA Modules:
  0.0 75.5 jit_solution(1840036063555345153)
XLA Ops:
  0.6 72.3 %shard_map.85 = (f32[3,256]{1,0:T(4,128)}, f32[3,256]{1,0:T(4,128)}, f32[2,128]{1,0:T(2,128)}) custom-call(f32[3,256]{1,0:T(4,128)} %pos_ref.1, f32[6,3,256]{2,1,0:T(4,128)} %force_ref.1, f32[6,3,256]{2,1,0:T(4,128)} %kick_ref.1, f32[3,128,256]{2,1,0:T(8,128)} %bitcast.3, f32[3,128,256]{2,1,0:T(8,128)} %bitcast.4, s32[1,128]{1,0:T(1,128)} %bitcast.5), custom_call_target="tpu_custom_call" | custom-call | tf_op jit(solution)/shard_map/pallas_call | solution.py:298
  72.9 0.0 copy-start.1
  72.9 0.7 copy-done.1
  73.6 0.0 copy-start
  73.6 0.6 copy.12
  74.2 0.1 copy-done
  74.3 0.0 copy-start.2
  74.3 0.6 copy.13
  74.9 0.1 copy-done.2
  74.9 0.6 copy.14
Async XLA Ops:
  72.9 0.7 copy-start.1
  73.6 0.7 copy-start
  74.3 0.7 copy-start.2

commit v3 on v2

--- a/solution.py
+++ b/solution.py
@@ -9,7 +9,7 @@
 
 TIME_STEP = 0.05
 LANES = 128
-ROWS = 64
+ROWS = 128
 
 
 def pieces(value):

time: 75.8 us -> 74.8 us (0.987)
  Pallas kernels: 72.3 us -> 71.3 us
    pallas_call x1, Pallas kernels: 72.3 us -> 71.3 us  [local(): pl.pallas_call(functools.partial(kernel, n, steps), out_shape=(jax.ShapeD...]
where the time goes in v3:
time: 74.8 us; the launch traced here: 74.5 us
  Pallas kernels  71.3 us (95%)
  local copies, waits for them, and re-layouts  2.57 us (3%)
    pallas_call x1, Pallas kernels, local(): pl.pallas_call(functools.partial(kernel, n, steps), out_shape=(jax.ShapeD...  71.3 us
    unnamed x9, local copies, waits for them, and re-layouts  2.57 us

profile of v3, /device:TPU:0, one launch (start us, length us, event | category | flops | bytes accessed | tf_op | source)
XLA Modules:
  0.0 74.5 jit_solution(7316964755448192885)
XLA Ops:
  0.6 71.3 %shard_map.85 = (f32[3,256]{1,0:T(4,128)}, f32[3,256]{1,0:T(4,128)}, f32[2,128]{1,0:T(2,128)}) custom-call(f32[3,256]{1,0:T(4,128)} %pos_ref.1, f32[6,3,256]{2,1,0:T(4,128)} %force_ref.1, f32[6,3,256]{2,1,0:T(4,128)} %kick_ref.1, f32[3,128,256]{2,1,0:T(8,128)} %bitcast.3, f32[3,128,256]{2,1,0:T(8,128)} %bitcast.4, s32[1,128]{1,0:T(1,128)} %bitcast.5), custom_call_target="tpu_custom_call" | custom-call | tf_op jit(solution)/shard_map/pallas_call | solution.py:298
  72.0 0.0 copy-start.1
  72.0 0.7 copy-done.1
  72.6 0.0 copy-start
  72.6 0.6 copy.12
  73.2 0.1 copy-done
  73.3 0.0 copy-start.2
  73.3 0.6 copy.13
  73.9 0.1 copy-done.2
  74.0 0.6 copy.14
Async XLA Ops:
  72.0 0.7 copy-start.1
  72.6 0.7 copy-start
  73.3 0.7 copy-start.2
